TPU v7x, 32 devices: a whole 2x2x4 slice. The times are simulated.
32 devices in a mesh: gy: 4 (over x, core), gx: 8 (over z, y).
Axes of the slice: x: 2, y: 2, z: 4, core: 2. Of those that a mesh axis runs over, the one named last changes fastest.
Arguments:
- model_field: float32 [60, 1024, 1024], P(None, 'gy', 'gx'), may hold values from -160 to 160
- driver_field: float32 [60, 1024, 1024], P(None, 'gy', 'gx'), may hold values from -60 to 60
- nudge_rate: float32 [60], replicated, may hold values from 0.1 to 0.5
- increment_cap: float32 [60], replicated, may hold values from 1 to 3
Outputs:
- nudged: float32 [60, 1024, 1024], P(None, 'gy', 'gx')
All inputs are finite; a program needn't handle non-finite values.
Results may differ from a plain program's by a relative error of at most 0.00005.
Values sent between devices are 32-bit elements; how exact they have to be, the bound alone decides.
A program may use at most 64 MiB of HBM per device.

v0:
```python
import math

import jax
import jax.numpy as jnp
from jax import lax
from jax.sharding import PartitionSpec as P

MODES = 24


epsilon = 1e-06


def basis_table(cell_count, start, length_all):
    positions = start + lax.iota(jnp.int32, cell_count)
    wavenumber = jnp.concatenate([lax.iota(jnp.int32, MODES), lax.iota(jnp.int32, MODES) + 1])
    phases = positions[:, None] * wavenumber[None, :] % length_all
    angles = phases.astype(jnp.float32) * (2.0 * math.pi / length_all)
    column = lax.iota(jnp.int32, 2 * MODES)
    weights = jnp.where(column == 0, math.sqrt(1.0 / length_all), math.sqrt(2.0 / length_all))
    return jnp.where(column[None, :] < MODES, jnp.cos(angles), jnp.sin(angles)) * weights[None, :]


def per_device(model_field, driver_field, nudge_rate, increment_cap):
    highest = lax.Precision.HIGHEST
    fields, rows, columns = model_field.shape
    row_total = rows * lax.axis_size("gy")
    column_total = columns * lax.axis_size("gx")
    basis_rows = basis_table(rows, lax.axis_index("gy") * rows, row_total)
    basis_columns = basis_table(columns, lax.axis_index("gx") * columns, column_total)
    difference = driver_field - model_field
    local_squares = jnp.sum(difference * difference, axis=(1, 2))
    squares = lax.psum(local_squares, ("gy", "gx"))
    extra = ()

    def over_columns(source):
        return jnp.einsum("fyx,xk->fyk", source, basis_columns, precision=highest)

    def over_rows(partial_value):
        return jnp.einsum("yj,fyk->fjk", basis_rows, partial_value, precision=highest)

    sources = (difference,)
    count = len(sources)
    summed = lax.psum(
        tuple((over_rows(over_columns(source)) for source in sources)) + extra, ("gy", "gx")
    )
    coefficients = summed[0]
    spread = jnp.sqrt(squares / (row_total * column_total) + epsilon)
    strength = nudge_rate * jnp.minimum(1.0, increment_cap / spread)
    rows_part = jnp.einsum("yj,fjk->fyk", basis_rows, coefficients, precision=highest)
    large_scale = jnp.einsum("fyk,xk->fyx", rows_part, basis_columns, precision=highest)
    return model_field + strength[:, None, None] * large_scale


def solution(mesh):
    return jax.shard_map(
        per_device,
        mesh=mesh,
        in_specs=(P(None, "gy", "gx"), P(None, "gy", "gx"), P(), P()),
        out_specs=P(None, "gy", "gx"),
        check_vma=False,
    )
```

profile of v0, /device:TPU:0, one launch (start us, length us, event | category | flops | bytes accessed | tf_op | source)
XLA Modules:
  0.0 186.3 jit_solution(12665342513090759011)
XLA Ops:
  6.5 0.0 all-reduce.2.cloned.1.call-start
  6.6 0.1 pad_add_fusion
  6.7 12.4 %fusion = f32[60,256,48]{1,2,0:T(8,128)S(1)} fusion(f32[60,256,128]{2,1,0:T(8,128)} %param.5, f32[60,256,128]{2,1,0:T(8,128)} %param.4, f32[48]{0:T(128)S(1)} %compare_select_fusion, s32[48]{0:T(128)S(1)} %pad_add_fusion, s32[128]{0:T(128)S(1)} %iota_add_fusion.2, pred[48]{0:T(512)(128)(4,1)S(1)} %iota_compare_fusion), kind=kOutput, calls=%fused_computation.2 | convolution fusion | flops 1134526464 | bytes 18678704 | tf_op jit(solution)/shard_map/fyx,xk->fyk/dot_general | solution.py:37
  19.1 4.2 %convolution_bitcast_fusion = f32[60,48,48]{1,2,0:T(8,128)} fusion(f32[60,256,48]{1,2,0:T(8,128)S(1)} %fusion, f32[48]{0:T(128)S(1)} %compare_select_fusion, s32[48]{0:T(128)S(1)} %pad_add_fusion, s32[256]{0:T(256)S(1)} %iota_add_fusion, pred[48]{0:T(512)(128)(4,1)S(1)} %iota_compare_fusion), kind=kOutput, calls=%fused_computation.5 | convolution fusion | flops 424869888 | bytes 3503536 | tf_op jit(solution)/shard_map/yj,fyk->fjk/dot_general | solution.py:40
  23.3 0.0 all-reduce.2.cloned.1.call-update
  23.3 0.0 copy-start
  23.3 0.0 copy-start.1
  23.3 6.7 %multiply_reduce_fusion = f32[60]{0:T(128)S(1)} fusion(f32[60,256,128]{2,1,0:T(8,128)} %param.5, f32[60,256,128]{2,1,0:T(8,128)} %param.4), kind=kLoop, calls=%fused_computation.1 | loop fusion | flops 5898180 | bytes 15728880 | tf_op jit(solution)/shard_map/reduce_sum | solution.py:32
  30.0 42.2 %psum.14 = f32[60]{0:T(128)S(1)} all-reduce(f32[60]{0:T(128)S(1)} %multiply_reduce_fusion), channel_id=1, replica_groups=mesh['gy'=4,'gx'=8] {'gy','gx'}, use_global_device_ids=true, to_apply=%region_1.2 | all-reduce | flops 60 | bytes 480 | tf_op jit(solution)/shard_map/psum | solution.py:33
  72.2 0.0 copy-done
  72.2 0.0 copy-done.1
  72.2 85.6 %all-reduce.2.cloned.1.call-done = f32[60,48,48]{1,2,0:T(8,128)} async-done(((f32[60,48,48]{1,2,0:T(8,128)}), f32[60,48,48]{1,2,0:T(8,128)}) %all-reduce.2.cloned.1.call-update) | async-done | bytes 552976 | tf_op jit(solution)/shard_map/psum | solution.py:44
  157.9 4.4 %fusion.6 = f32[60,48,256]{2,1,0:T(8,128)S(1)} fusion(f32[60,48,48]{1,2,0:T(8,128)} %all-reduce.2.cloned.1.call-done, f32[48]{0:T(128)S(1)} %compare_select_fusion, s32[48]{0:T(128)S(1)} %pad_add_fusion, s32[256]{0:T(256)S(1)} %iota_add_fusion, pred[48]{0:T(512)(128)(4,1)S(1)} %iota_compare_fusion), kind=kOutput, calls=%fused_computation.14 | convolution fusion | flops 424869888 | bytes 3503536 | tf_op jit(solution)/shard_map/yj,fjk->fyk/dot_general | solution.py:50
  162.3 17.2 %multiply_add_fusion = f32[60,256,128]{2,1,0:T(8,128)} fusion(f32[60,256,128]{2,1,0:T(8,128)} %param.4, f32[60]{0:T(128)S(1)} %minimum_multiply_fusion, f32[60,48,256]{2,1,0:T(8,128)S(1)} %fusion.6, f32[48]{0:T(128)S(1)} %compare_select_fusion, s32[48]{0:T(128)S(1)} %pad_add_fusion, s32[128]{0:T(128)S(1)} %iota_add_fusion.2, pred[48]{0:T(512)(128)(4,1)S(1)} %iota_compare_fusion), kind=kOutput, calls=%fused_computation | convolution fusion | flops 1136492544 | bytes 18678944 | tf_op jit(solution)/shard_map/fyk,xk->fyx/dot_general | solution.py:51
  (7 shorter events, 0.0 us)
Async XLA Ops:
  6.5 151.3 %all-reduce.2.cloned.1.call-start = ((), (), s32[]{:S(2)}) async-start(), calls=%async_computation | async-start | bytes 2949120 | tf_op jit(solution)/shard_map/psum | solution.py:44
  23.3 48.9 %copy-start = (f32[60]{0:T(128)S(1)}, f32[60]{0:T(128)}, u32[]{:S(2)}) copy-start(f32[60]{0:T(128)} %param.6) | copy-start | bytes 724
  23.3 48.9 %copy-start.1 = (f32[60]{0:T(128)S(1)}, f32[60]{0:T(128)}, u32[]{:S(2)}) copy-start(f32[60]{0:T(128)} %param.7) | copy-start | bytes 724
Sparse Core Ops, SparseCore 0:
  23.4 134.3 all-reduce.1
where the time goes:
time: 187 us; the launch traced here: 186 us
  waiting for transfers between devices  85.7 us (46%)
  blocking collectives  42.2 us (23%)
  matrix products  38.2 us (20%)
  between operations  13.5 us (7%)
  other arithmetic  6.82 us (4%)
    psum x1, waiting for transfers between devices, per_device(): lax.psum(tuple((over_rows(over_columns(source)) for source in sources)) +...  85.6 us
    psum x1, blocking collectives, per_device(): squares = lax.psum(local_squares, ('gy', 'gx'))  42.2 us
    dot_general x1, matrix products, per_device(): jnp.einsum('fyk,xk->fyx', rows_part, basis_columns, precision=highest)  17.2 us
    dot_general x1, matrix products, over_columns(): return jnp.einsum('fyx,xk->fyk', source, basis_columns, precision=highest)  12.4 us
    reduce_sum x1, other arithmetic, per_device(): local_squares = jnp.sum(difference * difference, axis=(1, 2))  6.71 us
    dot_general x1, matrix products, per_device(): jnp.einsum('yj,fjk->fyk', basis_rows, coefficients, precision=highest)  4.43 us
    dot_general x1, matrix products, over_rows(): jnp.einsum('yj,fyk->fjk', basis_rows, partial_value, precision=highest)  4.16 us
  transfers between devices with their start and end apart: 1, of which 1 were waited for; matrix products, arithmetic and copies ran while one was open for 4% of the time, Pallas kernels for 0%

commit v1 on v0

v1 whole, which is shorter than its diff:
```python
import functools
import math

import jax
import jax.numpy as jnp
import numpy as np
from jax import lax
from jax.experimental import pallas as pl
from jax.experimental.pallas import tpu as pltpu
from jax.sharding import PartitionSpec as P

MODES = 24
KEPT = 2 * MODES
HALF = 64
LANES = 2 * HALF
EPSILON = 1e-06
FIELDS_STEP = 4
SLOTS_CHUNK = 2
MESH = pl.DeviceIdType.MESH
F32, BF16 = jnp.float32, jnp.bfloat16


def split(value):
    high = value.astype(BF16)
    return high, (value - high.astype(F32)).astype(BF16)


def dot(a, b):
    return jnp.dot(a, b, preferred_element_type=F32)


def basis_table(length):
    position = np.arange(length)[:, None]
    number = np.concatenate([np.arange(MODES), np.arange(MODES) + 1])[None, :]
    angle = (position * number % length) * (2.0 * math.pi / length)
    column = np.arange(KEPT)[None, :]
    weight = np.where(column == 0, math.sqrt(1.0 / length), math.sqrt(2.0 / length))
    table = (np.where(column < MODES, np.cos(angle), np.sin(angle)) * weight).astype(np.float32)
    high = table.astype(BF16)
    return high, (table - high.astype(np.float32)).astype(BF16)


def tables(row_total, column_total, ny, nx):
    rows, columns = row_total // ny, column_total // nx
    yh, yl = (part.reshape(ny, rows, KEPT) for part in basis_table(row_total))
    xh, xl = (part.reshape(nx, columns, KEPT) for part in basis_table(column_total))
    gap = np.zeros((nx, columns, HALF - KEPT), BF16)
    twice = [np.concatenate([part, gap, part, gap], axis=2) for part in (xh, xl)]
    x_in = np.stack(twice, axis=1)
    x_out = np.ascontiguousarray(np.swapaxes(x_in, 2, 3))
    y_in = np.ascontiguousarray(np.swapaxes(np.concatenate([yh, yl], axis=2), 1, 2))
    y_out = np.concatenate([yh, yh, yl], axis=2)
    return y_in, x_in, y_out, x_out


def owner_x(slot, nx):
    return (slot % SLOTS_CHUNK) * (nx // SLOTS_CHUNK) + slot // SLOTS_CHUNK


def analysis_kernel(
    ny, nx, cells,
    model, driver, y_table, x_table, rate, cap, full,
    model_v, driver_v, y_v, x_v, weight, coef, from_y, row_sum, from_x,
    in_sem, table_sem, send_y, recv_y, send_x, recv_x,
    gather_x_send, gather_x_recv, gather_y_send, gather_y_recv, core_send, core_recv,
):
    fields, rows, columns = model.shape
    my_y, my_x = lax.axis_index("gy"), lax.axis_index("gx")
    pairs, steps = fields // 2, fields // FIELDS_STEP
    chunk_pairs = SLOTS_CHUNK * ny
    chunk_steps = chunk_pairs // 2
    chunks = nx // SLOTS_CHUNK

    def load(step):
        part = pl.ds(step * FIELDS_STEP, FIELDS_STEP)
        return (
            pltpu.make_async_copy(model.at[part], model_v.at[part], in_sem.at[step, 0]),
            pltpu.make_async_copy(driver.at[part], driver_v.at[part], in_sem.at[step, 1]),
        )

    table_copies = (
        pltpu.make_async_copy(y_table.at[my_y], y_v, table_sem.at[0]),
        pltpu.make_async_copy(x_table.at[my_x], x_v, table_sem.at[1]),
    )
    for copy in table_copies:
        copy.start()

    @pl.loop(0, steps)
    def _(step):
        for copy in load(step):
            copy.start()

    barrier = pltpu.get_barrier_semaphore()
    for k in range(1, ny):
        pl.semaphore_signal(
            barrier, inc=1, device_id=(lax.rem(my_y + k, ny), my_x), device_id_type=MESH
        )
    for k in range(1, nx):
        pl.semaphore_signal(
            barrier, inc=1, device_id=(my_y, lax.rem(my_x + k, nx)), device_id_type=MESH
        )

    for pair in range(pairs, ny * nx):
        coef[pair % ny, pair // ny] = jnp.zeros((KEPT, LANES), F32)
    for copy in table_copies:
        copy.wait()
    lane_w = lax.broadcasted_iota(jnp.int32, (columns, LANES), 1)
    for part, order in ((0, (0, 2)), (1, (1,))):
        value = x_v[part].astype(F32)
        left = jnp.where(lane_w < HALF, value, 0.0).astype(BF16)
        right = jnp.where(lane_w < HALF, 0.0, value).astype(BF16)
        for at in ((0, 1), (2,))[part]:
            weight[pl.ds(at * columns, columns)] = left
            weight[pl.ds((3 + at) * columns, columns)] = right

    lane = lax.broadcasted_iota(jnp.int32, (8, LANES), 1)

    def compute(step):
        for copy in load(step):
            copy.wait()
        sums, squares = [], []
        for pair in range(FIELDS_STEP // 2):
            blocks, marks = [], jnp.zeros((8, LANES), F32)
            for field in range(2):
                at = step * FIELDS_STEP + pair * 2 + field
                difference = driver_v[at] - model_v[at]
                high, low = split(difference)
                blocks += [high, low, high]
                part = jnp.sum((difference * difference).reshape(rows // 8, 8, columns), axis=0)
                mark = jnp.sum(part, axis=1, keepdims=True)
                marks = jnp.where(lane == field * HALF + KEPT, mark, marks)
            sums.append(dot(jnp.concatenate(blocks, axis=1), weight[...]))
            squares.append(marks)
        high, low = split(jnp.concatenate(sums, axis=1))
        first = dot(y_v[...], high)
        found = first[:KEPT] + first[KEPT:] + dot(y_v[:KEPT], low)
        for pair in range(FIELDS_STEP // 2):
            at = step * (FIELDS_STEP // 2) + pair
            g, q = lax.rem(at, ny), lax.div(at, ny)
            block = found[:, pair * LANES:(pair + 1) * LANES]
            coef[g, q, 0:8] = block[0:8] + squares[pair]
            coef[g, q, 8:KEPT] = block[8:]

    def to_rows(chunk, k):
        part = pl.ds(chunk * SLOTS_CHUNK, SLOTS_CHUNK)
        target = lax.rem(my_y + k, ny)
        return pltpu.make_async_remote_copy(
            src_ref=coef.at[target, part], dst_ref=from_y.at[k - 1, part],
            send_sem=send_y.at[chunk, k - 1], recv_sem=recv_y.at[chunk, k - 1],
            device_id=(target, my_x), device_id_type=MESH,
        )

    def to_owner(slot):
        target = owner_x(slot, nx)
        offset = lax.rem(my_x - target + nx, nx)
        return pltpu.make_async_remote_copy(
            src_ref=row_sum.at[slot], dst_ref=from_x.at[offset],
            send_sem=send_x.at[slot], recv_sem=recv_x.at[offset],
            device_id=(my_y, target), device_id_type=MESH,
        )

    def finish(chunk):
        for k in range(1, ny):
            to_rows(chunk, k).wait_recv()
        for slot in range(chunk * SLOTS_CHUNK, (chunk + 1) * SLOTS_CHUNK):
            total = coef[my_y, slot]
            for k in range(1, ny):
                total += from_y[k - 1, slot]
            row_sum[slot] = total

            @pl.when(my_x != owner_x(slot, nx))
            def _():
                to_owner(slot).start()

    for chunk in range(chunks):
        low, high = (min(steps, part * chunk_steps) for part in (chunk, chunk + 1))
        if high > low:
            pl.loop(low, high)(compute)
        if chunk == 0:
            pl.semaphore_wait(barrier, ny + nx - 2)
        for k in range(1, ny):
            to_rows(chunk, k).start()
        if chunk > 0:
            finish(chunk - 1)
    finish(chunks - 1)

    my_slot = lax.rem(my_x, nx // SLOTS_CHUNK) * SLOTS_CHUNK + lax.div(my_x, nx // SLOTS_CHUNK)
    my_pair = my_slot * ny + my_y
    total = row_sum[my_slot]
    for k in range(1, nx):
        pltpu.make_async_remote_copy(
            src_ref=row_sum.at[0], dst_ref=from_x.at[k],
            send_sem=send_x.at[0], recv_sem=recv_x.at[k],
            device_id=(my_y, lax.rem(my_x + k, nx)), device_id_type=MESH,
        ).wait_recv()
        total += from_x[k]
    lane_c = lax.broadcasted_iota(jnp.int32, (KEPT, LANES), 1)
    strength = []
    for field in range(2):
        at = jnp.minimum(my_pair * 2 + field, fields - 1)
        mark = jnp.where(lane_c == field * HALF + KEPT, total, 0.0)
        square = jnp.sum(jnp.sum(mark, axis=0, keepdims=True), axis=1, keepdims=True)
        spread = jnp.sqrt(square / cells + EPSILON)
        strength.append(rate[at] * jnp.minimum(1.0, cap[at] / spread))
    scale = jnp.where(lane_c < HALF, strength[0], strength[1])
    full[my_y, my_x] = jnp.where(lane_c % HALF < KEPT, total * scale, 0.0)

    half_y = ny // 2
    partner = my_y + 1 - 2 * lax.rem(my_y, 2)

    def x_of(k):
        return lax.rem(my_x - k + nx, nx)

    def y_of(j):
        return lax.rem(my_y - 2 * j + ny, ny)

    def gather_x(k):
        return pltpu.make_async_remote_copy(
            src_ref=full.at[my_y, my_x], dst_ref=full.at[my_y, my_x],
            send_sem=gather_x_send.at[k], recv_sem=gather_x_recv.at[k],
            device_id=(my_y, lax.rem(my_x + k, nx)), device_id_type=MESH,
        )

    def gather_y(j, k):
        return pltpu.make_async_remote_copy(
            src_ref=full.at[my_y, x_of(k)], dst_ref=full.at[my_y, x_of(k)],
            send_sem=gather_y_send.at[j, k], recv_sem=gather_y_recv.at[j, k],
            device_id=(lax.rem(my_y + 2 * j, ny), my_x), device_id_type=MESH,
        )

    def to_core(j, k):
        return pltpu.make_async_remote_copy(
            src_ref=full.at[y_of(j), x_of(k)], dst_ref=full.at[y_of(j), x_of(k)],
            send_sem=core_send.at[j, k], recv_sem=core_recv.at[j, k],
            device_id=(partner, my_x), device_id_type=MESH,
        )

    for k in range(1, nx):
        gather_x(k).start()
    for k in range(nx):
        if k:
            gather_x(k).wait_recv()
        for j in range(1, half_y):
            gather_y(j, k).start()
        to_core(0, k).start()
    for k in range(nx):
        for j in range(1, half_y):
            gather_y(j, k).wait_recv()
            to_core(j, k).start()
    for k in range(nx):
        for j in range(half_y):
            to_core(j, k).wait_recv()

    for chunk in range(chunks):
        for k in range(1, ny):
            to_rows(chunk, k).wait_send()
    for slot in range(nx):
        @pl.when(my_x != owner_x(slot, nx))
        def _():
            to_owner(slot).wait_send()
    for k in range(nx):
        if k:
            gather_x(k).wait_send()
        for j in range(half_y):
            if j:
                gather_y(j, k).wait_send()
            to_core(j, k).wait_send()


def build_kernel(ny, nx, model, full, y_table, x_table, out, y_v, x_v, weight, table_sem):
    step = pl.program_id(0)
    columns = model.shape[2]

    @pl.when(step == 0)
    def _():
        copies = (
            pltpu.make_async_copy(y_table.at[lax.axis_index("gy")], y_v, table_sem.at[0]),
            pltpu.make_async_copy(x_table.at[lax.axis_index("gx")], x_v, table_sem.at[1]),
        )
        for copy in copies:
            copy.start()
        for copy in copies:
            copy.wait()
        row = lax.broadcasted_iota(jnp.int32, (LANES, columns), 0)
        for part in range(2):
            value = x_v[part].astype(F32)
            left = jnp.where(row < HALF, value, 0.0).astype(BF16)
            right = jnp.where(row < HALF, 0.0, value).astype(BF16)
            both = jnp.concatenate([left, right], axis=1)
            for at in ((0, 1), (2,))[part]:
                weight[pl.ds(at * LANES, LANES)] = both

    for pair in range(FIELDS_STEP // 2):
        at = step * (FIELDS_STEP // 2) + pair
        high, low = split(full[lax.rem(at, ny), owner_x(lax.div(at, ny), nx)])
        along = dot(y_v[...], jnp.concatenate([high, low, high], axis=0))
        high, low = split(along)
        large = dot(jnp.concatenate([high, low, high], axis=1), weight[...])
        out[2 * pair] = model[2 * pair] + large[:, :columns]
        out[2 * pair + 1] = model[2 * pair + 1] + large[:, columns:]


def per_device(ny, nx, model, driver, rate, cap):
    fields, rows, columns = model.shape
    assert fields % FIELDS_STEP == 0 and fields // 2 <= ny * nx
    assert ny % 2 == 0 and nx % SLOTS_CHUNK == 0
    row_total, column_total = rows * ny, columns * nx
    y_in, x_in, y_out, x_out = (
        jnp.asarray(table) for table in tables(row_total, column_total, ny, nx)
    )
    anywhere = pl.BlockSpec(memory_space=pl.ANY)
    scalars = pl.BlockSpec(memory_space=pltpu.SMEM)
    vector = pl.BlockSpec(memory_space=pltpu.VMEM)
    dma = pltpu.SemaphoreType.DMA
    chunks, half_y = nx // SLOTS_CHUNK, ny // 2
    full = pl.pallas_call(
        functools.partial(analysis_kernel, ny, nx, float(row_total * column_total)),
        out_shape=jax.ShapeDtypeStruct((ny, nx, KEPT, LANES), F32),
        in_specs=[anywhere, anywhere, anywhere, anywhere, scalars, scalars],
        out_specs=vector,
        scratch_shapes=[
            pltpu.VMEM((fields, rows, columns), F32),
            pltpu.VMEM((fields, rows, columns), F32),
            pltpu.VMEM((2 * KEPT, rows), BF16),
            pltpu.VMEM((2, columns, LANES), BF16),
            pltpu.VMEM((6 * columns, LANES), BF16),
            pltpu.VMEM((ny, nx, KEPT, LANES), F32),
            pltpu.VMEM((ny - 1, nx, KEPT, LANES), F32),
            pltpu.VMEM((nx, KEPT, LANES), F32),
            pltpu.VMEM((nx, KEPT, LANES), F32),
            dma((fields // FIELDS_STEP, 2)), dma((2,)),
            dma((chunks, ny - 1)), dma((chunks, ny - 1)), dma((nx,)), dma((nx,)),
            dma((nx,)), dma((nx,)), dma((half_y, nx)), dma((half_y, nx)),
            dma((half_y, nx)), dma((half_y, nx)),
        ],
        compiler_params=pltpu.CompilerParams(
            collective_id=0, has_side_effects=True, vmem_limit_bytes=60 * 2**20
        ),
        name="analysis",
    )(model, driver, y_in, x_in, rate, cap)
    block = pl.BlockSpec((FIELDS_STEP, rows, columns), lambda i: (i, 0, 0))
    return pl.pallas_call(
        functools.partial(build_kernel, ny, nx),
        grid=(fields // FIELDS_STEP,),
        out_shape=jax.ShapeDtypeStruct(model.shape, F32),
        in_specs=[block, vector, anywhere, anywhere],
        out_specs=block,
        scratch_shapes=[
            pltpu.VMEM((rows, 3 * KEPT), BF16),
            pltpu.VMEM((2, LANES, columns), BF16),
            pltpu.VMEM((3 * LANES, 2 * columns), BF16),
            dma((2,)),
        ],
        compiler_params=pltpu.CompilerParams(
            dimension_semantics=("arbitrary",), vmem_limit_bytes=60 * 2**20
        ),
        name="build",
    )(model, full, y_out, x_out)


def solution(mesh):
    return jax.shard_map(
        functools.partial(per_device, mesh.shape["gy"], mesh.shape["gx"]),
        mesh=mesh,
        in_specs=(P(None, "gy", "gx"), P(None, "gy", "gx"), P(), P()),
        out_specs=P(None, "gy", "gx"),
        check_vma=False,
    )
```

time: 187 us -> 51.5 us (0.28)
  waiting for transfers between devices: 85.7 us -> 0 us
  Pallas kernels: 0 us -> 51.1 us
  blocking collectives: 42.2 us -> 0 us
  matrix products: 38.2 us -> 0 us
  between operations: 13.5 us -> 0.01 us
  other arithmetic: 6.82 us -> 0 us
    psum x1 -> x0, waiting for transfers between devices: 85.6 us -> none  [per_device(): lax.psum(tuple((over_rows(over_columns(source)) for source in sources)) +...]
    pallas_call x0 -> x2, Pallas kernels: none -> 51.1 us  [the longest x1 35.6 us: per_device(): pl.pallas_call(functools.partial(analysis_kernel, ny, nx, float(row_total...]
    psum x1 -> x0, blocking collectives: 42.2 us -> none  [per_device(): squares = lax.psum(local_squares, ('gy', 'gx'))]
    dot_general x4 -> x0, matrix products: 38.2 us -> none  [the longest x1 17.2 us: per_device(): jnp.einsum('fyk,xk->fyx', rows_part, basis_columns, precision=highest)]
    reduce_sum x1 -> x0, other arithmetic: 6.71 us -> none  [per_device(): local_squares = jnp.sum(difference * difference, axis=(1, 2))]
  transfers between devices with their start and end apart: 1 -> 0, of which waited for: 1 -> 0; matrix products, arithmetic and copies ran while one was open for 4% -> 0% of each run, Pallas kernels for 0% -> 0%
where the time goes in v1:
time: 51.5 us; the launch traced here: 51.1 us
  Pallas kernels  51.1 us (99%)
    pallas_call x1, Pallas kernels, per_device(): pl.pallas_call(functools.partial(analysis_kernel, ny, nx, float(row_total...  35.6 us
    pallas_call x1, Pallas kernels, per_device(): pl.pallas_call(functools.partial(build_kernel, ny, nx), grid=(fields // F...  15.5 us

profile of v1, /device:TPU:0, one launch (start us, length us, event | category | flops | bytes accessed | tf_op | source)
XLA Modules:
  0.0 51.1 jit_solution(8853507037988925941)
XLA Ops:
  0.0 35.6 %analysis.1.full = f32[4,8,48,128]{3,2,1,0:T(8,128)} custom-call(f32[60,256,128]{2,1,0:T(8,128)} %model.3, f32[60,256,128]{2,1,0:T(8,128)} %driver.1, bf16[4,96,256]{2,1,0:T(8,128)(2,1)} %constant.8.clone.y_table, bf16[8,2,128,128]{3,2,1,0:T(8,128)(2,1)} %constant.9.clone.x_table, f32[60]{0:T(128)} %rate.1, f32[60]{0:T(128)} %cap.1), custom_call_target="tpu_custom_call" | custom-call | tf_op jit(solution)/shard_map/analysis/pallas_call | solution.py:316
  35.6 15.5 %build.1 = f32[60,256,128]{2,1,0:T(8,128)} custom-call(f32[60,256,128]{2,1,0:T(8,128)} %model.3, f32[4,8,48,128]{3,2,1,0:T(8,128)} %analysis.1.full, bf16[4,256,144]{2,1,0:T(8,128)(2,1)} %constant.10.clone.y_table, bf16[8,2,128,128]{3,2,1,0:T(8,128)(2,1)} %constant.11.clone.x_table), custom_call_target="tpu_custom_call" | custom-call | tf_op jit(solution)/shard_map/build/pallas_call | solution.py:342

commit v2 on v1

--- a/solution.py
+++ b/solution.py
@@ -15,7 +15,10 @@
 LANES = 2 * HALF
 EPSILON = 1e-06
 FIELDS_STEP = 4
+BUILD_STEP = 12
 SLOTS_CHUNK = 2
+VMEM_BYTES = 67_043_328
+VMEM_SPARE = 2**16
 MESH = pl.DeviceIdType.MESH
 F32, BF16 = jnp.float32, jnp.bfloat16
 
@@ -59,8 +62,8 @@
 
 def analysis_kernel(
     ny, nx, cells,
-    model, driver, y_table, x_table, rate, cap, full,
-    model_v, driver_v, y_v, x_v, weight, coef, from_y, row_sum, from_x,
+    model, driver, y_table, x_table, rate_in, cap_in, full, model_v,
+    driver_v, rate, cap, y_v, x_v, weight, coef, from_y, row_sum, from_x,
     in_sem, table_sem, send_y, recv_y, send_x, recv_x,
     gather_x_send, gather_x_recv, gather_y_send, gather_y_recv, core_send, core_recv,
 ):
@@ -81,6 +84,8 @@
     table_copies = (
         pltpu.make_async_copy(y_table.at[my_y], y_v, table_sem.at[0]),
         pltpu.make_async_copy(x_table.at[my_x], x_v, table_sem.at[1]),
+        pltpu.make_async_copy(rate_in, rate, table_sem.at[2]),
+        pltpu.make_async_copy(cap_in, cap, table_sem.at[3]),
     )
     for copy in table_copies:
         copy.start()
@@ -290,37 +295,40 @@
             for at in ((0, 1), (2,))[part]:
                 weight[pl.ds(at * LANES, LANES)] = both
 
-    for pair in range(FIELDS_STEP // 2):
-        at = step * (FIELDS_STEP // 2) + pair
+    for pair in range(BUILD_STEP // 2):
+        at = step * (BUILD_STEP // 2) + pair
         high, low = split(full[lax.rem(at, ny), owner_x(lax.div(at, ny), nx)])
         along = dot(y_v[...], jnp.concatenate([high, low, high], axis=0))
         high, low = split(along)
         large = dot(jnp.concatenate([high, low, high], axis=1), weight[...])
-        out[2 * pair] = model[2 * pair] + large[:, :columns]
-        out[2 * pair + 1] = model[2 * pair + 1] + large[:, columns:]
+        out[2 * pair] = model[2 * at] + large[:, :columns]
+        out[2 * pair + 1] = model[2 * at + 1] + large[:, columns:]
 
 
 def per_device(ny, nx, model, driver, rate, cap):
     fields, rows, columns = model.shape
-    assert fields % FIELDS_STEP == 0 and fields // 2 <= ny * nx
+    assert fields % FIELDS_STEP == fields % BUILD_STEP == 0 and fields // 2 <= ny * nx
     assert ny % 2 == 0 and nx % SLOTS_CHUNK == 0
     row_total, column_total = rows * ny, columns * nx
     y_in, x_in, y_out, x_out = (
         jnp.asarray(table) for table in tables(row_total, column_total, ny, nx)
     )
     anywhere = pl.BlockSpec(memory_space=pl.ANY)
-    scalars = pl.BlockSpec(memory_space=pltpu.SMEM)
+    hbm = pl.BlockSpec(memory_space=pltpu.HBM)
     vector = pl.BlockSpec(memory_space=pltpu.VMEM)
     dma = pltpu.SemaphoreType.DMA
     chunks, half_y = nx // SLOTS_CHUNK, ny // 2
-    full = pl.pallas_call(
+    kept = 4 * (fields * rows * columns + ny * nx * KEPT * LANES)
+    room = VMEM_BYTES - kept - VMEM_SPARE
+    full, model_kept = pl.pallas_call(
         functools.partial(analysis_kernel, ny, nx, float(row_total * column_total)),
-        out_shape=jax.ShapeDtypeStruct((ny, nx, KEPT, LANES), F32),
-        in_specs=[anywhere, anywhere, anywhere, anywhere, scalars, scalars],
-        out_specs=vector,
+        out_shape=(pltpu.VMEM((ny, nx, KEPT, LANES), F32), pltpu.VMEM(model.shape, F32)),
+        in_specs=[hbm] * 6,
+        out_specs=(vector, vector),
         scratch_shapes=[
             pltpu.VMEM((fields, rows, columns), F32),
-            pltpu.VMEM((fields, rows, columns), F32),
+            pltpu.SMEM((fields,), F32),
+            pltpu.SMEM((fields,), F32),
             pltpu.VMEM((2 * KEPT, rows), BF16),
             pltpu.VMEM((2, columns, LANES), BF16),
             pltpu.VMEM((6 * columns, LANES), BF16),
@@ -328,22 +336,22 @@
             pltpu.VMEM((ny - 1, nx, KEPT, LANES), F32),
             pltpu.VMEM((nx, KEPT, LANES), F32),
             pltpu.VMEM((nx, KEPT, LANES), F32),
-            dma((fields // FIELDS_STEP, 2)), dma((2,)),
+            dma((fields // FIELDS_STEP, 2)), dma((4,)),
             dma((chunks, ny - 1)), dma((chunks, ny - 1)), dma((nx,)), dma((nx,)),
             dma((nx,)), dma((nx,)), dma((half_y, nx)), dma((half_y, nx)),
             dma((half_y, nx)), dma((half_y, nx)),
         ],
         compiler_params=pltpu.CompilerParams(
-            collective_id=0, has_side_effects=True, vmem_limit_bytes=60 * 2**20
+            collective_id=0, has_side_effects=True, vmem_limit_bytes=room
         ),
         name="analysis",
     )(model, driver, y_in, x_in, rate, cap)
-    block = pl.BlockSpec((FIELDS_STEP, rows, columns), lambda i: (i, 0, 0))
+    block = pl.BlockSpec((BUILD_STEP, rows, columns), lambda i: (i, 0, 0))
     return pl.pallas_call(
         functools.partial(build_kernel, ny, nx),
-        grid=(fields // FIELDS_STEP,),
+        grid=(fields // BUILD_STEP,),
         out_shape=jax.ShapeDtypeStruct(model.shape, F32),
-        in_specs=[block, vector, anywhere, anywhere],
+        in_specs=[vector, vector, anywhere, anywhere],
         out_specs=block,
         scratch_shapes=[
             pltpu.VMEM((rows, 3 * KEPT), BF16),
@@ -352,10 +360,10 @@
             dma((2,)),
         ],
         compiler_params=pltpu.CompilerParams(
-            dimension_semantics=("arbitrary",), vmem_limit_bytes=60 * 2**20
+            dimension_semantics=("arbitrary",), vmem_limit_bytes=36 * 2**20
         ),
         name="build",
-    )(model, full, y_out, x_out)
+    )(model_kept, full, y_out, x_out)
 
 
 def solution(mesh):

time: 51.5 us -> 43 us (0.83)
  Pallas kernels: 51.1 us -> 40.7 us
  local copies, waits for them, and re-layouts: 0 us -> 2.08 us
    pallas_call x1, Pallas kernels: 15.5 us -> 6.68 us  [per_device(): pl.pallas_call(functools.partial(build_kernel, ny, nx), grid=(fields // B...]
    unnamed x0 -> x4, local copies, waits for them, and re-layouts: none -> 2.08 us
    pallas_call x1, Pallas kernels: 35.6 us -> 34 us  [per_device(): pl.pallas_call(functools.partial(analysis_kernel, ny, nx, float(row_total...]
where the time goes in v2:
time: 43 us; the launch traced here: 42.8 us
  Pallas kernels  40.7 us (95%)
  local copies, waits for them, and re-layouts  2.08 us (5%)
    pallas_call x1, Pallas kernels, per_device(): pl.pallas_call(functools.partial(analysis_kernel, ny, nx, float(row_total...  34 us
    pallas_call x1, Pallas kernels, per_device(): pl.pallas_call(functools.partial(build_kernel, ny, nx), grid=(fields // B...  6.68 us
    unnamed x4, local copies, waits for them, and re-layouts  2.08 us

profile of v2, /device:TPU:0, one launch (start us, length us, event | category | flops | bytes accessed | tf_op | source)
XLA Modules:
  0.0 42.8 jit_solution(10315368852050161590)
XLA Ops:
  0.0 34.0 %analysis.1 = (f32[4,8,48,128]{3,2,1,0:T(8,128)S(1)}, f32[60,256,128]{2,1,0:T(8,128)S(1)}) custom-call(f32[60,256,128]{2,1,0:T(8,128)} %model.1, f32[60,256,128]{2,1,0:T(8,128)} %driver.1, bf16[4,96,256]{2,1,0:T(8,128)(2,1)} %constant.8.clone.y_table, bf16[8,2,128,128]{3,2,1,0:T(8,128)(2,1)} %constant.9.clone.x_table, f32[60]{0:T(128)} %rate_in.1, f32[60]{0:T(128)} %cap_in.1), custom_call_target="tpu_custom_call" | custom-call | tf_op jit(solution)/shard_map/analysis/pallas_call | solution.py:323
  34.0 0.0 copy-start
  34.1 1.0 %copy-done = bf16[8,2,128,128]{3,2,1,0:T(8,128)(2,1)S(1)} copy-done((bf16[8,2,128,128]{3,2,1,0:T(8,128)(2,1)S(1)}, bf16[8,2,128,128]{3,2,1,0:T(8,128)(2,1)}, u32[]{:S(2)}) %copy-start) | copy-done | bytes 524312
  35.1 0.0 copy-start.1
  35.1 1.0 %copy-done.1 = bf16[4,256,144]{2,1,0:T(8,128)(2,1)S(1)} copy-done((bf16[4,256,144]{2,1,0:T(8,128)(2,1)S(1)}, bf16[4,256,144]{2,1,0:T(8,128)(2,1)}, u32[]{:S(2)}) %copy-start.1) | copy-done | bytes 294936
  36.1 6.7 %build.1 = f32[60,256,128]{2,1,0:T(8,128)} custom-call(f32[60,256,128]{2,1,0:T(8,128)S(1)} %get-tuple-element.7.model, f32[4,8,48,128]{3,2,1,0:T(8,128)S(1)} %get-tuple-element.8.full, bf16[4,256,144]{2,1,0:T(8,128)(2,1)S(1)} %copy-done.1, bf16[8,2,128,128]{3,2,1,0:T(8,128)(2,1)S(1)} %copy-done), custom_call_target="tpu_custom_call" | custom-call | tf_op jit(solution)/shard_map/build/pallas_call | solution.py:350
Async XLA Ops:
  34.0 1.0 %copy-start = (bf16[8,2,128,128]{3,2,1,0:T(8,128)(2,1)S(1)}, bf16[8,2,128,128]{3,2,1,0:T(8,128)(2,1)}, u32[]{:S(2)}) copy-start(bf16[8,2,128,128]{3,2,1,0:T(8,128)(2,1)} %constant.11.clone.x_table) | copy-start | bytes 1572868
  35.1 1.0 %copy-start.1 = (bf16[4,256,144]{2,1,0:T(8,128)(2,1)S(1)}, bf16[4,256,144]{2,1,0:T(8,128)(2,1)}, u32[]{:S(2)}) copy-start(bf16[4,256,144]{2,1,0:T(8,128)(2,1)} %constant.10.clone.y_table) | copy-start | bytes 884740
